TPU v7x, 256 devices: a whole 4x4x8 slice. The times are simulated.
256 devices in a mesh: dp: 32 (over x, y, core), tensor: 8 (over z).
Axes of the slice: x: 4, y: 4, z: 8, core: 2. Of those that a mesh axis runs over, the one named last changes fastest.
Arguments:
- query: bfloat16 [512, 4096], P('dp', 'tensor'), may hold values from -8000 to 8000
- incoming_key: bfloat16 [512, 2048], P('dp', 'tensor'), may hold values from -4.5 to 4.5
- new_value: bfloat16 [512, 2048], P('dp', 'tensor'), may hold values from -4.5 to 4.5
- key_cache: bfloat16 [512, 256, 2048], P('dp', None, 'tensor'), may hold values from -4.5 to 4.5
- value_cache: bfloat16 [512, 256, 2048], P('dp', None, 'tensor'), may hold values from -4.5 to 4.5
- cache_len: int32 [512], P('dp'), may hold values from 2 to 256
- out_weight: bfloat16 [4096, 4608], P('tensor'), may hold values from -0.09375 to 0.09375
- residual: bfloat16 [512, 4608], P('dp'), may hold values from -6 to 6
- post_gain: float32 [4608], replicated, may hold values from 0.5 to 1.5
- final_gain: float32 [4608], replicated, may hold values from 0.5 to 1.5
- vocab_weight: bfloat16 [131072, 4608], P(('dp', 'tensor')), may hold values from -113 to 113
- sampled: int32 [512], P('dp'), may hold values from 0 to 131071
- stop_flag: int32 [512], P('dp'), may hold values from 0 to 1, as said below
Outputs:
- new_residual: bfloat16 [512, 4608], P('dp', 'tensor')
- token_logprob: float32 [512], P('dp')
- insert_rank: int32 [512], P('dp')
- released_slot_total: int32 [], replicated
Inputs may be any that keep to these rules, and one draw needn't show every extreme that they name: `stop_flag`: each aligned block of 16 slots holds 1 to 16 stops.
All inputs are finite; a program needn't handle non-finite values.
Results may differ from a plain program's by a relative error of at most 0.0038.
The roundings to bfloat16 on the way count: a program that leaves them out, or rounds other values in their place, can miss the bound.
Values may be sent and summed in bfloat16 or wider, within the bound.
No kernel may reach another device: no remote copies, remote signals or barrier semaphores. Data moves between devices by JAX's collectives and lax.ppermute only.
A program may use at most 64 MiB of HBM per device.

v0:
```python
import jax
import jax.numpy as jnp
from jax import lax
from jax.sharding import Mesh
from jax.sharding import PartitionSpec as P

D = 4608
HEADS = 32
KV_HEADS = 16
HEAD_DIM = 128
DP = ("dp_0", "dp_1", "dp_2")
DP_TENSOR = ("dp_0", "dp_1", "dp_2", "tensor")


def gathered_total(shard, axis):
    return lax.all_gather(shard, axis).sum(0)


def all_in_one(shard, axis):
    leaves = jax.tree.leaves(shard)
    sequence = sorted(range(len(leaves)), key=lambda k: -leaves[k].size)
    width = (1, *leaves[sequence[0]].shape)[-1]
    lines = [
        jnp.pad(leaves[k].reshape(-1), (0, -leaves[k].size % width)).reshape(-1, width)
        for k in sequence
    ]
    both, at, found = (lax.all_gather(jnp.concatenate(lines), axis), 0, {})
    for k, line in zip(sequence, lines):
        share = both[:, at : at + len(line)].reshape(len(both), -1)
        found[k] = share[:, : leaves[k].size].reshape(-1, *leaves[k].shape)
        at += len(line)
    numbers = iter(range(len(leaves)))
    return jax.tree.map(lambda _: found[next(numbers)], shard)


def combined_by_axis(shard, axes, combine):
    for axis in axes:
        pieces = all_in_one(shard, axis)
        shard = jax.tree.map(lambda part: part[0], pieces)
        for k in range(1, lax.axis_size(axis)):
            shard = combine(shard, jax.tree.map(lambda part: part[k], pieces))
    return shard


def attend_local(query, incoming_key, new_value, key_cache, value_cache, cache_len):
    slot_dev = query.shape[0]
    positions = key_cache.shape[1]
    kv_local = incoming_key.shape[1] // HEAD_DIM
    group = HEADS // KV_HEADS
    query_vector = query.reshape(slot_dev, kv_local, group, HEAD_DIM)
    keys = key_cache.reshape(slot_dev, positions, kv_local, HEAD_DIM)
    values = value_cache.reshape(slot_dev, positions, kv_local, HEAD_DIM)
    self_key = incoming_key.reshape(slot_dev, kv_local, HEAD_DIM)
    own_value = new_value.reshape(slot_dev, kv_local, HEAD_DIM).astype(jnp.float32)
    scores = (
        jnp.einsum("bkgd,bckd->bkgc", query_vector, keys, preferred_element_type=jnp.float32) / 12.0
    )
    self_entry = (
        jnp.einsum("qyxm,qym->qyx", query_vector, self_key, preferred_element_type=jnp.float32)
        / 12.0
    )
    valid = (
        jnp.arange(positions, dtype=jnp.int32)[None, None, None, :] < cache_len[:, None, None, None]
    )
    scores = jnp.where(valid, scores, -1e30)
    top = jnp.maximum(jnp.max(scores, axis=-1), self_entry)
    expo = jnp.where(valid, jnp.exp(scores - top[..., None]), 0.0)
    own_exp = jnp.exp(self_entry - top)
    total = jnp.sum(expo, axis=-1) + own_exp
    weight = (expo / total[..., None]).astype(jnp.bfloat16)
    own_weight = (own_exp / total).astype(jnp.bfloat16).astype(jnp.float32)
    attn = jnp.einsum("bkgc,bckd->bkgd", weight, values, preferred_element_type=jnp.float32)
    attn = attn + own_weight[..., None] * own_value[:, :, None, :]
    return attn.astype(jnp.bfloat16).reshape(slot_dev, kv_local * group * HEAD_DIM)


def collect_slots(hidden, sampled):
    return (
        lax.all_gather(hidden, DP, axis=0, tiled=True),
        lax.all_gather(sampled, DP, axis=0, tiled=True),
    )


def combine_stats(first, second):
    top = jnp.maximum(first[0], second[0])
    total = first[1] * jnp.exp(first[0] - top) + second[1] * jnp.exp(second[0] - top)
    return (top, total, first[2] + second[2], first[3] + second[3])


def on_device(
    query,
    incoming_key,
    new_value,
    key_cache,
    value_cache,
    cache_len,
    out_weight,
    residual,
    post_gain,
    final_gain,
    vocab_weight,
    sampled,
    stop_flag,
):
    slot_dev = query.shape[0]
    attn = attend_local(query, incoming_key, new_value, key_cache, value_cache, cache_len)
    partial_value = jnp.dot(attn, out_weight, preferred_element_type=jnp.float32)
    whole = gathered_total(partial_value, "tensor")
    post = whole * lax.rsqrt(jnp.mean(whole * whole, axis=1, keepdims=True) + 1e-06) * post_gain
    full_mix = (residual.astype(jnp.float32) + post).astype(jnp.bfloat16)
    mixed = full_mix.astype(jnp.float32)
    hidden = (
        mixed * lax.rsqrt(jnp.mean(mixed * mixed, axis=1, keepdims=True) + 1e-06) * final_gain
    ).astype(jnp.bfloat16)
    width = D // lax.axis_size("tensor")
    new_residual = lax.dynamic_slice_in_dim(full_mix, lax.axis_index("tensor") * width, width, 1)
    every, ids = collect_slots(hidden, sampled)
    logits = lax.dot_general(
        every, vocab_weight, (((1,), (1,)), ((), ())), preferred_element_type=jnp.float32
    )
    vocabulary_per_device = vocab_weight.shape[0]
    vocab_start = (
        lax.axis_index(DP) * lax.axis_size("tensor") + lax.axis_index("tensor")
    ) * vocabulary_per_device
    local_ids = ids - vocab_start
    hit = jnp.arange(vocabulary_per_device, dtype=jnp.int32)[None, :] == local_ids[:, None]
    picked_part = jnp.sum(jnp.where(hit, logits, 0.0), axis=1)
    row_max = jnp.max(logits, axis=1)
    freed = (stop_flag == 1).astype(jnp.int32)
    count = jnp.sum(freed)
    groups = lax.axis_size(DP)
    lane_ids = jnp.arange(groups, dtype=jnp.int32)
    first_core = (lax.axis_index("tensor") == 0).astype(jnp.float32)
    lanes = jnp.where(lane_ids == lax.axis_index(DP), count.astype(jnp.float32) * first_core, 0.0)
    local_sum = jnp.sum(jnp.exp(logits - row_max[:, None]), axis=1)
    top, expsum, picked, tallied_entries = combined_by_axis(
        (row_max, local_sum, picked_part, lanes), DP_TENSOR, combine_stats
    )
    before = jnp.sum(jnp.where(lane_ids < lax.axis_index(DP), tallied_entries, 0.0)).astype(
        jnp.int32
    )
    released_count = jnp.sum(tallied_entries).astype(jnp.int32)
    logprob_all = picked - (jnp.log(expsum) + top)
    token_logprob = lax.dynamic_slice_in_dim(
        logprob_all, lax.axis_index(DP) * slot_dev, slot_dev, 0
    )
    local_before = jnp.cumsum(freed) - freed + before
    insert_rank = jnp.where(freed == 1, local_before, -1)
    return (new_residual, token_logprob, insert_rank, released_count)


def solution(mesh):
    split = Mesh(
        mesh.devices.reshape(4, 4, 2, mesh.shape["tensor"]), ("dp_0", "dp_1", "dp_2", "tensor")
    )
    in_specs = (
        P(DP, "tensor"),
        P(DP, "tensor"),
        P(DP, "tensor"),
        P(DP, None, "tensor"),
        P(DP, None, "tensor"),
        P(DP),
        P("tensor", None),
        P(DP, None),
        P(),
        P(),
        P(DP_TENSOR, None),
        P(DP),
        P(DP),
    )
    out_specs = (P(DP, "tensor"), P(DP), P(DP), P())
    return jax.shard_map(
        on_device, mesh=split, in_specs=in_specs, out_specs=out_specs, check_vma=False
    )
```

profile of v0, /device:TPU:2, one launch (start us, length us, event | category | flops | bytes accessed | tf_op | source)
XLA Modules:
  0.0 184.3 jit_solution(2291557467032989353)
XLA Ops:
  7.2 0.0 copy-start
  7.2 0.0 copy-start.4
  7.2 0.0 all-gather.14.cloned.1.call-start
  7.2 0.9 reshape.784
  8.1 0.7 reshape.834
  8.8 0.7 iota_compare_fusion.1
  9.5 0.1 fusion.85
  9.7 0.0 copy-done
  9.7 0.7 fusion.83
  10.5 0.2 fusion.22
  10.7 0.0 copy-done.4
  10.8 2.0 %fusion.15 = bf16[16,2,2,128]{3,2,1,0:T(2,128)(2,1)S(1)} fusion(f32[16,2,2]{2,1,0:T(2,128)S(1)} %get-tuple-element.34, f32[16,2,128]{2,1,0:T(2,128)S(1)} %reshape.802, f32[16,2,2]{2,1,0:T(2,128)S(1)} %get-tuple-element.33, f32[16,2,2,256]{3,2,1,0:T(2,128)S(1)} %get-tuple-element.36, pred[16,256]{1,0:T(8,128)(4,1)S(1)} %iota_compare_fusion.1, ...), kind=kOutput, calls=%fused_computation.9 | convolution fusion | flops 4284416 | bytes 2200320 | tf_op jit(solution)/shard_map/bkgc,bckd->bkgd/dot_general | solution.py:72
  12.8 3.8 %fusion.86 = f32[16,4608]{1,0:T(8,128)} fusion(bf16[16,512]{1,0:T(8,128)(2,1)S(1)} %reshape.788, bf16[512,4608]{1,0:T(8,128)(2,1)} %param.19), kind=kOutput, calls=%fused_computation.160 | convolution fusion | flops 75497472 | bytes 5029888 | tf_op jit(solution)/shard_map/dot_general | solution.py:107
  16.6 0.0 copy-start.1
  16.6 0.0 copy-start.2
  16.6 0.0 copy-start.3
  16.6 0.0 all-gather.14.cloned.1.call-update
  16.6 0.0 copy-start.5
  16.7 0.0 copy-start.7
  16.7 0.0 copy-start.6
  16.7 0.0 all-gather.12.cloned.1.call-start
  16.7 44.2 %all-gather.14.cloned.1.call-done = f32[128,4608]{1,0:T(8,128)} async-done(((f32[16,4608]{1,0:T(8,128)}), f32[128,4608]{1,0:T(8,128)}) %all-gather.14.cloned.1.call-update) | async-done | bytes 2359312 | tf_op jit(solution)/shard_map/all_gather | solution.py:16
  60.9 1.8 reduce_sum.82
  62.8 0.2 multiply_reduce_fusion
  62.9 0.0 copy-done.1
  62.9 0.0 copy-done.2
  62.9 0.3 fusion.18
  63.2 0.0 copy-done.3
  63.2 0.8 fusion.20
  64.0 0.0 all-gather.12.cloned.1.call-update
  64.0 0.0 copy-done.5
  64.0 0.6 fusion.74
  65.4 0.1 copy.25
  65.5 0.1 reduce.1
  65.6 0.0 copy-done.7
  65.6 0.6 dynamic-slice
  66.9 0.0 copy-done.6
  66.9 0.2 dynamic-update-slice
  67.1 15.3 %all-reduce.4 = s32[512]{0:T(512)S(1)} all-reduce(s32[512]{0:T(512)S(1)} %dynamic-update-slice), channel_id=1, replica_groups=mesh['dp_0'=4,'dp_1'=4,'dp_2'=2,'tensor'=8] {'dp_0','dp_1','dp_2'}, use_global_device_ids=true, to_apply=%add.4 | all-reduce | flops 512 | bytes 4096
  82.5 0.7 constant_dynamic-slice_fusion
  83.1 31.1 %all-gather.12.cloned.1.call-done = bf16[512,4608]{1,0:T(8,128)(2,1)} async-done(((bf16[16,4608]{1,0:T(8,128)(2,1)}), bf16[512,4608]{1,0:T(8,128)(2,1)}) %all-gather.12.cloned.1.call-update) | async-done | bytes 4718608 | tf_op jit(solution)/shard_map/all_gather | solution.py:79
  114.2 5.9 %fusion.84 = (f32[512]{0:T(512)S(1)}, f32[512,512]{0,1:T(8,128)S(1)}) fusion(bf16[512,4608]{1,0:T(8,128)(2,1)} %all-gather.12.cloned.1.call-done, bf16[512,4608]{1,0:T(8,128)(2,1)} %param.23), kind=kOutput, calls=%fused_computation.158 | convolution fusion | flops 2416180736 | bytes 10487808 | tf_op jit(solution)/shard_map/dot_general | solution.py:118
  120.2 0.3 exponential_reduce_fusion
  120.5 11.9 %all-gather.5 = f32[4,4,512]{2,1,0:T(4,128)S(1)} all-gather(f32[1,4,512]{2,1,0:T(4,128)S(1)} %maximum_bitcast_fusion), channel_id=3, replica_groups=mesh['dp_0'=4,'dp_1'=4,'dp_2'=2,'tensor'=8] {'dp_0'}, dimensions={0}, use_global_device_ids=true | all-gather | bytes 40960 | tf_op jit(solution)/shard_map/all_gather | solution.py:27
  132.5 11.9 %all-gather.6 = f32[4,4,512]{2,1,0:T(4,128)S(1)} all-gather(f32[1,4,512]{2,1,0:T(4,128)S(1)} %maximum_bitcast_fusion.1), channel_id=4, replica_groups=mesh['dp_0'=4,'dp_1'=4,'dp_2'=2,'tensor'=8] {'dp_1'}, dimensions={0}, use_global_device_ids=true | all-gather | bytes 40960 | tf_op jit(solution)/shard_map/all_gather | solution.py:27
  144.6 1.8 all-gather.7
  146.5 26.0 %all-gather.8 = f32[8,4,512]{2,1,0:T(4,128)S(1)} all-gather(f32[1,4,512]{2,1,0:T(4,128)S(1)} %maximum_bitcast_fusion.3), channel_id=6, replica_groups=mesh['dp_0'=4,'dp_1'=4,'dp_2'=2,'tensor'=8] {'tensor'}, dimensions={0}, use_global_device_ids=true | all-gather | bytes 73728 | tf_op jit(solution)/shard_map/all_gather | solution.py:27
  172.6 0.6 fusion.77
  173.2 0.6 fusion.69
  175.2 0.6 dynamic_slice.7
  175.8 0.5 compare_select_fusion.1
  (39 shorter events, 0.5 us)
Async XLA Ops:
  7.2 2.5 %copy-start = (bf16[16,256,256]{2,1,0:T(8,128)(2,1)S(1)}, bf16[16,256,256]{2,1,0:T(8,128)(2,1)}, u32[]{:S(2)}) copy-start(bf16[16,256,256]{2,1,0:T(8,128)(2,1)} %param.16) | copy-start | bytes 6291460
  7.2 3.5 %copy-start.4 = (bf16[16,256]{1,0:T(8,128)(2,1)S(1)}, bf16[16,256]{1,0:T(8,128)(2,1)}, u32[]{:S(2)}) copy-start(bf16[16,256]{1,0:T(8,128)(2,1)} %param.15) | copy-start | bytes 24580
  7.2 53.7 %all-gather.14.cloned.1.call-start = ((), (), s32[]{:S(2)}) async-start(), calls=%async_computation.1 | async-start | bytes 2654208 | tf_op jit(solution)/shard_map/all_gather | solution.py:16
  16.6 46.3 %copy-start.1 = (bf16[16,4608]{1,0:T(8,128)(2,1)S(1)}, bf16[16,4608]{1,0:T(8,128)(2,1)}, u32[]{:S(2)}) copy-start(bf16[16,4608]{1,0:T(8,128)(2,1)} %param.20) | copy-start | bytes 442372
  16.6 46.3 %copy-start.2 = (f32[4608]{0:T(1024)S(1)}, f32[4608]{0:T(1024)}, u32[]{:S(2)}) copy-start(f32[4608]{0:T(1024)} %param.21) | copy-start | bytes 55300
  16.6 46.6 %copy-start.3 = (f32[4608]{0:T(1024)S(1)}, f32[4608]{0:T(1024)}, u32[]{:S(2)}) copy-start(f32[4608]{0:T(1024)} %param.22) | copy-start | bytes 55300
  16.6 47.4 %copy-start.5 = (s32[16]{0:T(128)S(1)}, s32[16]{0:T(128)}, u32[]{:S(2)}) copy-start(s32[16]{0:T(128)} %param.25) | copy-start | bytes 196
  16.7 49.0 %copy-start.7 = (u32[256]{0:T(256)S(1)}, u32[256]{0:T(256)}, u32[]{:S(2)}) copy-start(u32[256]{0:T(256)} %constant.77) | copy-start | bytes 3076
  16.7 50.2 %copy-start.6 = (s32[16]{0:T(128)S(1)}, s32[16]{0:T(128)}, u32[]{:S(2)}) copy-start(s32[16]{0:T(128)} %param.24) | copy-start | bytes 196
  16.7 97.6 %all-gather.12.cloned.1.call-start = ((), (), s32[]{:S(2)}) async-start(), calls=%async_computation | async-start | bytes 4866048 | tf_op jit(solution)/shard_map/all_gather | solution.py:79
Sparse Core Ops, SparseCore 0:
  16.8 44.1 all-gather.13
  64.1 50.0 all-gather.11
where the time goes:
time: 185 us; the launch traced here: 184 us
  waiting for transfers between devices  75.3 us (41%)
  blocking collectives  67 us (36%)
  between operations  18.2 us (10%)
  matrix products  12.6 us (7%)
  other arithmetic  7.08 us (4%)
  local copies, waits for them, and re-layouts  3.94 us (2%)
    all_gather x4, blocking collectives, all_in_one(): both, at, found = (lax.all_gather(jnp.concatenate(lines), axis), 0, {})  51.7 us
    all_gather x1, waiting for transfers between devices, gathered_total(): return lax.all_gather(shard, axis).sum(0)  44.2 us
    all_gather x1, waiting for transfers between devices, collect_slots(): lax.all_gather(hidden, DP, axis=0, tiled=True)  31.1 us
    unnamed x1, blocking collectives  15.3 us
    dot_general x1, matrix products, on_device(): lax.dot_general(every, vocab_weight, (((1,), (1,)), ((), ())), preferred_...  5.93 us
    dot_general x1, matrix products, on_device(): jnp.dot(attn, out_weight, preferred_element_type=jnp.float32)  3.79 us
  transfers between devices with their start and end apart: 2, of which 2 were waited for; matrix products, arithmetic and copies ran while one was open for 1% of the time, Pallas kernels for 0%

commit v1 on v0

--- a/solution.py
+++ b/solution.py
@@ -76,7 +76,7 @@
 
 def collect_slots(hidden, sampled):
     return (
-        lax.all_gather(hidden, DP, axis=0, tiled=True),
+        jnp.concatenate(lax.all_to_all(jnp.stack([hidden] * lax.axis_size(DP)), DP, 0, 0), axis=0),
         lax.all_gather(sampled, DP, axis=0, tiled=True),
     )
 

time: 185 us -> 208 us (1.12)
  blocking collectives: 67 us -> 110 us
  waiting for transfers between devices: 75.3 us -> 44.3 us
  starting transfers between devices: 0.08 us -> 7.63 us
  local copies, waits for them, and re-layouts: 3.94 us -> 6.63 us
    unnamed x1, blocking collectives: 15.3 us -> 60.9 us
    all_gather x1 -> x0, waiting for transfers between devices: 31.1 us -> none  [collect_slots(): lax.all_gather(hidden, DP, axis=0, tiled=True)]
    all_to_all x0 -> x1, starting transfers between devices: none -> 7.6 us  [collect_slots(): lax.all_to_all(jnp.stack([hidden] * lax.axis_size(DP)), DP, 0, 0)]
    another operation x1 -> x2, local copies, waits for them, and re-layouts: 0.08 us -> 2.78 us  [the longest x1 2.7 us: collect_slots(): jnp.stack([hidden] * lax.axis_size(DP))]
    all_gather x4, blocking collectives: 51.7 us -> 49.1 us  [all_in_one(): both, at, found = (lax.all_gather(jnp.concatenate(lines), axis), 0, {})]
  transfers between devices with their start and end apart: 2 -> 2, of which waited for: 2 -> 1; matrix products, arithmetic and copies ran while one was open for 1% -> 1% of each run, Pallas kernels for 0% -> 0%
where the time goes in v1:
time: 208 us; the launch traced here: 206 us
  blocking collectives  110 us (53%)
  waiting for transfers between devices  44.3 us (21%)
  between operations  18.1 us (9%)
  matrix products  12.6 us (6%)
  starting transfers between devices  7.63 us (4%)
  local copies, waits for them, and re-layouts  6.63 us (3%)
  other arithmetic  6.4 us (3%)
    unnamed x1, blocking collectives  60.9 us
    all_gather x4, blocking collectives, all_in_one(): both, at, found = (lax.all_gather(jnp.concatenate(lines), axis), 0, {})  49.1 us
    all_gather x1, waiting for transfers between devices, gathered_total(): return lax.all_gather(shard, axis).sum(0)  44.3 us
    all_to_all x1, starting transfers between devices, collect_slots(): lax.all_to_all(jnp.stack([hidden] * lax.axis_size(DP)), DP, 0, 0)  7.6 us
    dot_general x1, matrix products, on_device(): lax.dot_general(every, vocab_weight, (((1,), (1,)), ((), ())), preferred_...  5.93 us
  transfers between devices with their start and end apart: 2, of which 1 were waited for; matrix products, arithmetic and copies ran while one was open for 1% of the time, Pallas kernels for 0%

profile of v1, /device:TPU:2, one launch (start us, length us, event | category | flops | bytes accessed | tf_op | source)
XLA Modules:
  0.0 205.7 jit_solution(15334490493847468482)
XLA Ops:
  7.2 0.0 copy-start
  7.2 0.0 copy-start.4
  7.2 0.0 all-gather.11.cloned.1.call-start
  7.2 0.9 reshape.789
  8.1 0.7 reshape.840
  8.8 0.7 iota_compare_fusion.1
  9.5 0.1 fusion.85
  9.7 0.0 copy-done
  9.7 0.7 fusion.83
  10.5 0.2 fusion.22
  10.7 0.0 copy-done.4
  10.8 2.0 fusion.15
  12.8 3.8 %fusion.86 = f32[16,4608]{1,0:T(8,128)} fusion(bf16[16,512]{1,0:T(8,128)(2,1)S(1)} %reshape.793, bf16[512,4608]{1,0:T(8,128)(2,1)} %param.19), kind=kOutput, calls=%fused_computation.160 | convolution fusion | flops 75497472 | bytes 5029888 | tf_op jit(solution)/shard_map/dot_general | solution.py:107
  16.6 0.0 copy-start.1
  16.6 0.0 copy-start.2
  16.6 0.0 copy-start.3
  16.6 0.0 all-gather.11.cloned.1.call-update
  16.6 44.3 %all-gather.11.cloned.1.call-done = f32[128,4608]{1,0:T(8,128)} async-done(((f32[16,4608]{1,0:T(8,128)}), f32[128,4608]{1,0:T(8,128)}) %all-gather.11.cloned.1.call-update) | async-done | bytes 2359312 | tf_op jit(solution)/shard_map/all_gather | solution.py:16
  60.9 1.8 reduce_sum.82
  62.8 0.2 multiply_reduce_fusion
  62.9 0.0 copy-done.1
  62.9 0.0 copy-done.2
  62.9 0.3 fusion.18
  63.2 0.0 copy-done.3
  63.2 0.1 fusion.20
  63.3 2.7 %stack.2 = bf16[32,16,4608]{2,1,0:T(8,128)(2,1)} broadcast(bf16[16,4608]{1,0:T(8,128)(2,1)S(1)} %fusion.20), dimensions={1,2} | broadcast | bytes 4866048 | tf_op jit(solution)/shard_map/stack | solution.py:79
  66.0 0.0 copy-start.5
  66.0 0.0 copy-start.7
  66.0 0.0 copy-start.6
  66.0 7.6 %all-to-all-start = ((bf16[32,16,4608]{2,1,0:T(8,128)(2,1)}), bf16[32,16,4608]{2,1,0:T(8,128)(2,1)}, u32[]{:S(2)}, u32[]{:S(2)}) async-start(bf16[32,16,4608]{2,1,0:T(8,128)(2,1)} %stack.2), calls=%async_computation | async-start | bytes 9437184 | tf_op jit(solution)/shard_map/all_to_all | solution.py:79
  73.6 0.0 copy-done.5
  73.6 0.6 fusion.74
  75.0 0.1 copy.25
  75.1 0.1 reduce.1
  75.2 0.0 copy-done.7
  75.2 0.6 dynamic-slice
  76.5 0.0 copy-done.6
  76.5 0.2 dynamic-update-slice
  76.7 60.9 %all-reduce.4 = s32[512]{0:T(512)S(1)} all-reduce(s32[512]{0:T(512)S(1)} %dynamic-update-slice), channel_id=1, replica_groups=mesh['dp_0'=4,'dp_1'=4,'dp_2'=2,'tensor'=8] {'dp_0','dp_1','dp_2'}, use_global_device_ids=true, to_apply=%add.4 | all-reduce | flops 512 | bytes 4096
  137.6 0.7 constant_dynamic-slice_fusion
  138.3 0.0 all-to-all-done
  138.3 5.9 %fusion.84 = (f32[512]{0:T(512)S(1)}, f32[512,512]{0,1:T(8,128)S(1)}) fusion(bf16[512,4608]{1,0:T(8,128)(2,1)} %bitcast.3, bf16[512,4608]{1,0:T(8,128)(2,1)} %param.23), kind=kOutput, calls=%fused_computation.158 | convolution fusion | flops 2416180736 | bytes 10487808 | tf_op jit(solution)/shard_map/dot_general | solution.py:118
  144.2 0.3 exponential_reduce_fusion
  144.6 10.7 %all-gather.5 = f32[4,4,512]{2,1,0:T(4,128)S(1)} all-gather(f32[1,4,512]{2,1,0:T(4,128)S(1)} %maximum_bitcast_fusion), channel_id=3, replica_groups=mesh['dp_0'=4,'dp_1'=4,'dp_2'=2,'tensor'=8] {'dp_0'}, dimensions={0}, use_global_device_ids=true | all-gather | bytes 40960 | tf_op jit(solution)/shard_map/all_gather | solution.py:27
  155.4 11.9 %all-gather.6 = f32[4,4,512]{2,1,0:T(4,128)S(1)} all-gather(f32[1,4,512]{2,1,0:T(4,128)S(1)} %maximum_bitcast_fusion.1), channel_id=4, replica_groups=mesh['dp_0'=4,'dp_1'=4,'dp_2'=2,'tensor'=8] {'dp_1'}, dimensions={0}, use_global_device_ids=true | all-gather | bytes 40960 | tf_op jit(solution)/shard_map/all_gather | solution.py:27
  167.5 1.8 all-gather.7
  169.4 24.6 %all-gather.8 = f32[8,4,512]{2,1,0:T(4,128)S(1)} all-gather(f32[1,4,512]{2,1,0:T(4,128)S(1)} %maximum_bitcast_fusion.3), channel_id=6, replica_groups=mesh['dp_0'=4,'dp_1'=4,'dp_2'=2,'tensor'=8] {'tensor'}, dimensions={0}, use_global_device_ids=true | all-gather | bytes 73728 | tf_op jit(solution)/shard_map/all_gather | solution.py:27
  194.1 0.6 fusion.77
  194.7 0.6 fusion.69
  196.6 0.6 dynamic_slice.7
  197.2 0.5 compare_select_fusion.1
  (39 shorter events, 0.5 us)
Async XLA Ops:
  7.2 2.5 %copy-start = (bf16[16,256,256]{2,1,0:T(8,128)(2,1)S(1)}, bf16[16,256,256]{2,1,0:T(8,128)(2,1)}, u32[]{:S(2)}) copy-start(bf16[16,256,256]{2,1,0:T(8,128)(2,1)} %param.16) | copy-start | bytes 6291460
  7.2 3.5 %copy-start.4 = (bf16[16,256]{1,0:T(8,128)(2,1)S(1)}, bf16[16,256]{1,0:T(8,128)(2,1)}, u32[]{:S(2)}) copy-start(bf16[16,256]{1,0:T(8,128)(2,1)} %param.15) | copy-start | bytes 24580
  7.2 53.8 %all-gather.11.cloned.1.call-start = ((), (), s32[]{:S(2)}) async-start(), calls=%async_computation.1 | async-start | bytes 2654208 | tf_op jit(solution)/shard_map/all_gather | solution.py:16
  16.6 46.3 %copy-start.1 = (bf16[16,4608]{1,0:T(8,128)(2,1)S(1)}, bf16[16,4608]{1,0:T(8,128)(2,1)}, u32[]{:S(2)}) copy-start(bf16[16,4608]{1,0:T(8,128)(2,1)} %param.20) | copy-start | bytes 442372
  16.6 46.3 %copy-start.2 = (f32[4608]{0:T(1024)S(1)}, f32[4608]{0:T(1024)}, u32[]{:S(2)}) copy-start(f32[4608]{0:T(1024)} %param.21) | copy-start | bytes 55300
  16.6 46.6 %copy-start.3 = (f32[4608]{0:T(1024)S(1)}, f32[4608]{0:T(1024)}, u32[]{:S(2)}) copy-start(f32[4608]{0:T(1024)} %param.22) | copy-start | bytes 55300
  66.0 7.6 %copy-start.5 = (s32[16]{0:T(128)S(1)}, s32[16]{0:T(128)}, u32[]{:S(2)}) copy-start(s32[16]{0:T(128)} %param.25) | copy-start | bytes 196
  66.0 9.2 %copy-start.7 = (u32[256]{0:T(256)S(1)}, u32[256]{0:T(256)}, u32[]{:S(2)}) copy-start(u32[256]{0:T(256)} %constant.77) | copy-start | bytes 3076
  66.0 10.5 %copy-start.6 = (s32[16]{0:T(128)S(1)}, s32[16]{0:T(128)}, u32[]{:S(2)}) copy-start(s32[16]{0:T(128)} %param.24) | copy-start | bytes 196
  66.0 72.3 %all-to-all-start = ((bf16[32,16,4608]{2,1,0:T(8,128)(2,1)}), bf16[32,16,4608]{2,1,0:T(8,128)(2,1)}, u32[]{:S(2)}, u32[]{:S(2)}) async-start(bf16[32,16,4608]{2,1,0:T(8,128)(2,1)} %stack.2), calls=%async_computation | async-start | bytes 9437184 | tf_op jit(solution)/shard_map/all_to_all | solution.py:79
Sparse Core Ops, SparseCore 0:
  16.8 44.1 all-gather.10
